TPU v7x, 32 devices: a whole 2x2x4 slice. The times are simulated.
32 devices in a mesh: gx: 4 (over x, core), gy: 4 (over z), gz: 2 (over y).
Axes of the slice: x: 2, y: 2, z: 4, core: 2. Of those that a mesh axis runs over, the one named last changes fastest.
Arguments:
- columns: int32 [1024, 2048], P(('gx', 'gy', 'gz')), may hold values from 0 to 32767, as said below
- counts: int32 [1024, 2048], P(('gx', 'gy', 'gz')), may hold values from 1 to 63
- nnz_count: int32 [1024], P(('gx', 'gy', 'gz')), may hold values from 1 to 2048, as said below
- selected: int32 [2048], replicated, may hold values from 0 to 32767, as said below
Outputs:
- gene_stats: float32 [2, 32768], P(None, 'gz')
- pca_input: bfloat16 [1024, 2048], P(('gx', 'gy'), 'gz')
Inputs may be any that keep to these rules, and one draw needn't show every extreme that they name: `columns`: in each row no two slots fall in the same block of 16 consecutive genes (so the first nnz_count slots hold distinct genes); slots beyond nnz_count are not part of the matrix. For every k, the live slots of one cell fall on at most 128 of the genes selected[k * 2048 / 2] to selected[(k + 1) * 2048 / 2 - 1]; some cell reaches 128 for every k in every draw. `nnz_count`: some cell has all 2048 slots live in every draw. `selected`: distinct genes.
All inputs are finite; a program needn't handle non-finite values.
Results may differ from a plain program's by a relative error of at most 0.0085.
Values may be sent and summed in bfloat16 or wider, within the bound.
A program may use at most 128 MiB of HBM per device.

v0:
```python
import jax
import jax.numpy as jnp
from jax import lax
from jax.sharding import PartitionSpec as P

GENES = 32768
SEL = 2048


target_sum = 10000.0
var_floor = 0.01
clip_value = 10.0
lane_count = 256


def standardize(dense, mean_sel, variance_sel):
    scale_sel = jnp.sqrt(jnp.maximum(variance_sel, var_floor))
    return jnp.clip((dense - mean_sel[None, :]) / scale_sel[None, :], -clip_value, clip_value)


def cell_block(pair):
    block_genes, block_values = pair
    high_count = GENES // lane_count
    high_ids = lax.broadcasted_iota(jnp.int32, (1, 1, high_count), 2)
    low_ids = lax.broadcasted_iota(jnp.int32, (1, 1, lane_count), 2)
    high_table = ((block_genes // lane_count)[:, :, None] == high_ids).astype(jnp.bfloat16)
    low_hit = (block_genes % lane_count)[:, :, None] == low_ids
    upper = lax.optimization_barrier(block_values.astype(jnp.bfloat16))
    lower = (block_values - upper.astype(jnp.float32)).astype(jnp.bfloat16)
    upper_table = jnp.where(low_hit, upper[:, :, None], jnp.bfloat16(0.0))
    lower_table = jnp.where(low_hit, lower[:, :, None], jnp.bfloat16(0.0))
    upper_part = jnp.einsum(
        "csh,csl->chl", high_table, upper_table, preferred_element_type=jnp.float32
    )
    lower_part = jnp.einsum(
        "csh,csl->chl", high_table, lower_table, preferred_element_type=jnp.float32
    )
    return upper_part + lower_part


def per_device(columns, counts, nnz_count, selected):
    local_cells = columns.shape[0]
    row_slots = columns.shape[1]
    owners = lax.axis_size("gz")
    owner_index = lax.axis_index("gz")
    cells = local_cells * lax.axis_size("gx") * lax.axis_size("gy") * owners
    slot = lax.broadcasted_iota(jnp.int32, counts.shape, 1)
    live = slot < nnz_count[:, None]
    raw = jnp.where(live, counts.astype(jnp.float32), jnp.float32(0.0))
    library = jnp.sum(raw, axis=1, keepdims=True)
    values = jnp.log1p(raw * (target_sum / library))
    genes = jnp.where(live, columns, 0)
    block_rows = 4
    block_total = local_cells // block_rows
    expanded = lax.map(
        cell_block,
        (
            genes.reshape(block_total, block_rows, row_slots),
            values.reshape(block_total, block_rows, row_slots),
        ),
    )
    expanded = expanded.reshape(local_cells, GENES)
    total = jnp.sum(expanded, axis=0)
    square = jnp.sum(expanded * expanded, axis=0)
    terms = jnp.stack([total, square])
    owned = GENES // owners
    sums = lax.psum(terms, ("gx", "gy", "gz"))
    own_sums = lax.dynamic_slice_in_dim(sums, owner_index * owned, owned, 1)
    picked_sums = jnp.take(sums, selected, axis=1)
    own_mean = own_sums[0] / cells
    own_variance = own_sums[1] / cells - own_mean * own_mean
    gene_stats = jnp.stack([own_mean, own_variance])
    sel_mean = picked_sums[0] / cells
    sel_variance = picked_sums[1] / cells - sel_mean * sel_mean
    dense = jnp.take(expanded, selected, axis=1)
    share_size = SEL // owners
    own_mean_sel = lax.dynamic_slice_in_dim(sel_mean, owner_index * share_size, share_size, 0)
    own_variance_sel = lax.dynamic_slice_in_dim(
        sel_variance, owner_index * share_size, share_size, 0
    )
    moved = lax.all_to_all(
        dense.astype(jnp.bfloat16), "gz", split_axis=1, concat_axis=0, tiled=True
    ).astype(dense.dtype)
    pca_input = standardize(moved, own_mean_sel, own_variance_sel).astype(jnp.bfloat16)
    return (gene_stats, pca_input)


def solution(mesh):
    return jax.shard_map(
        per_device,
        mesh=mesh,
        in_specs=(
            P(("gx", "gy", "gz"), None),
            P(("gx", "gy", "gz"), None),
            P(("gx", "gy", "gz")),
            P(),
        ),
        out_specs=(P(None, "gz"), P(("gx", "gy"), "gz")),
        check_vma=False,
    )
```

profile of v0, /device:TPU:0, one launch (start us, length us, event | category | flops | bytes accessed | tf_op | source)
XLA Modules:
  0.0 230.8 jit_solution(16225255947262282294)
XLA Ops:
  10.8 56.9 %while.12 = (s32[]{:T(128)}, f32[8,4,128,256]{3,2,1,0:T(8,128)}, s32[8,4,2048]{2,1,0:T(4,128)S(1)}, f32[8,4,2048]{2,1,0:T(4,128)S(1)}, s32[]{:T(128)}) while((s32[]{:T(128)}, f32[8,4,128,256]{3,2,1,0:T(8,128)}, s32[8,4,2048]{2,1,0:T(4,128)S(1)}, f32[8,4,2048]{2,1,0:T(4,128)S(1)}, s32[]{:T(128)}) %tuple.39), condition=%wide.region_2.3_spmd, body=%wide.region_1.2_spmd.sunk | while | flops 1084588032 | bytes 1982553 | solution.py:55
  10.9 3.2 %fusion.48 = f32[4,128,256]{2,1,0:T(8,128)S(1)} fusion(s32[4,2048]{1,0:T(4,128)S(1)} %add_select_fusion.5, bf16[4,2048]{1,0:T(4,128)(2,1)S(1)} %bitcast_convert_fusion.2, s32[4,2048]{1,0:T(4,128)S(1)} %get-tuple-element.109), kind=kOutput, calls=%fused_computation.5.clone.1 | convolution fusion | flops 542113792 | bytes 606208 | tf_op jit(solution)/shard_map/while/body/eval_jaxpr/csh,csl->chl/dot_general | solution.py:32
  14.1 3.8 %fusion.50 = f32[8,4,128,256]{3,2,1,0:T(8,128)} fusion(f32[8,4,128,256]{3,2,1,0:T(8,128)} %get-tuple-element.116, s32[]{:T(128)S(6)} %copy.30, f32[4,128,256]{2,1,0:T(8,128)S(1)} %fusion.48, s32[4,2048]{1,0:T(4,128)S(1)} %add_select_fusion.5, bf16[4,2048]{1,0:T(4,128)(2,1)S(1)} %fusion.49, s32[4,2048]{1,0:T(4,128)S(1)} %get-tuple-element.109), kind=kOutput, calls=%fused_computation.18.clone.1 | convolution fusion | flops 542244864 | bytes 1130500 | tf_op jit(solution)/shard_map/while/body/eval_jaxpr/csh,csl->chl/dot_general | solution.py:35
  18.0 3.2 %fusion.48 = f32[4,128,256]{2,1,0:T(8,128)S(1)} fusion(s32[4,2048]{1,0:T(4,128)S(1)} %add_select_fusion.5, bf16[4,2048]{1,0:T(4,128)(2,1)S(1)} %bitcast_convert_fusion.2, s32[4,2048]{1,0:T(4,128)S(1)} %get-tuple-element.109), kind=kOutput, calls=%fused_computation.5.clone.1 | convolution fusion | flops 542113792 | bytes 606208 | tf_op jit(solution)/shard_map/while/body/eval_jaxpr/csh,csl->chl/dot_general | solution.py:32
  21.2 3.8 %fusion.50 = f32[8,4,128,256]{3,2,1,0:T(8,128)} fusion(f32[8,4,128,256]{3,2,1,0:T(8,128)} %get-tuple-element.116, s32[]{:T(128)S(6)} %copy.30, f32[4,128,256]{2,1,0:T(8,128)S(1)} %fusion.48, s32[4,2048]{1,0:T(4,128)S(1)} %add_select_fusion.5, bf16[4,2048]{1,0:T(4,128)(2,1)S(1)} %fusion.49, s32[4,2048]{1,0:T(4,128)S(1)} %get-tuple-element.109), kind=kOutput, calls=%fused_computation.18.clone.1 | convolution fusion | flops 542244864 | bytes 1130500 | tf_op jit(solution)/shard_map/while/body/eval_jaxpr/csh,csl->chl/dot_general | solution.py:35
  25.1 3.2 %fusion.48 = f32[4,128,256]{2,1,0:T(8,128)S(1)} fusion(s32[4,2048]{1,0:T(4,128)S(1)} %add_select_fusion.5, bf16[4,2048]{1,0:T(4,128)(2,1)S(1)} %bitcast_convert_fusion.2, s32[4,2048]{1,0:T(4,128)S(1)} %get-tuple-element.109), kind=kOutput, calls=%fused_computation.5.clone.1 | convolution fusion | flops 542113792 | bytes 606208 | tf_op jit(solution)/shard_map/while/body/eval_jaxpr/csh,csl->chl/dot_general | solution.py:32
  28.3 3.8 %fusion.50 = f32[8,4,128,256]{3,2,1,0:T(8,128)} fusion(f32[8,4,128,256]{3,2,1,0:T(8,128)} %get-tuple-element.116, s32[]{:T(128)S(6)} %copy.30, f32[4,128,256]{2,1,0:T(8,128)S(1)} %fusion.48, s32[4,2048]{1,0:T(4,128)S(1)} %add_select_fusion.5, bf16[4,2048]{1,0:T(4,128)(2,1)S(1)} %fusion.49, s32[4,2048]{1,0:T(4,128)S(1)} %get-tuple-element.109), kind=kOutput, calls=%fused_computation.18.clone.1 | convolution fusion | flops 542244864 | bytes 1130500 | tf_op jit(solution)/shard_map/while/body/eval_jaxpr/csh,csl->chl/dot_general | solution.py:35
  32.3 3.2 %fusion.48 = f32[4,128,256]{2,1,0:T(8,128)S(1)} fusion(s32[4,2048]{1,0:T(4,128)S(1)} %add_select_fusion.5, bf16[4,2048]{1,0:T(4,128)(2,1)S(1)} %bitcast_convert_fusion.2, s32[4,2048]{1,0:T(4,128)S(1)} %get-tuple-element.109), kind=kOutput, calls=%fused_computation.5.clone.1 | convolution fusion | flops 542113792 | bytes 606208 | tf_op jit(solution)/shard_map/while/body/eval_jaxpr/csh,csl->chl/dot_general | solution.py:32
  35.4 3.8 %fusion.50 = f32[8,4,128,256]{3,2,1,0:T(8,128)} fusion(f32[8,4,128,256]{3,2,1,0:T(8,128)} %get-tuple-element.116, s32[]{:T(128)S(6)} %copy.30, f32[4,128,256]{2,1,0:T(8,128)S(1)} %fusion.48, s32[4,2048]{1,0:T(4,128)S(1)} %add_select_fusion.5, bf16[4,2048]{1,0:T(4,128)(2,1)S(1)} %fusion.49, s32[4,2048]{1,0:T(4,128)S(1)} %get-tuple-element.109), kind=kOutput, calls=%fused_computation.18.clone.1 | convolution fusion | flops 542244864 | bytes 1130500 | tf_op jit(solution)/shard_map/while/body/eval_jaxpr/csh,csl->chl/dot_general | solution.py:35
  39.4 3.2 %fusion.48 = f32[4,128,256]{2,1,0:T(8,128)S(1)} fusion(s32[4,2048]{1,0:T(4,128)S(1)} %add_select_fusion.5, bf16[4,2048]{1,0:T(4,128)(2,1)S(1)} %bitcast_convert_fusion.2, s32[4,2048]{1,0:T(4,128)S(1)} %get-tuple-element.109), kind=kOutput, calls=%fused_computation.5.clone.1 | convolution fusion | flops 542113792 | bytes 606208 | tf_op jit(solution)/shard_map/while/body/eval_jaxpr/csh,csl->chl/dot_general | solution.py:32
  42.5 3.8 %fusion.50 = f32[8,4,128,256]{3,2,1,0:T(8,128)} fusion(f32[8,4,128,256]{3,2,1,0:T(8,128)} %get-tuple-element.116, s32[]{:T(128)S(6)} %copy.30, f32[4,128,256]{2,1,0:T(8,128)S(1)} %fusion.48, s32[4,2048]{1,0:T(4,128)S(1)} %add_select_fusion.5, bf16[4,2048]{1,0:T(4,128)(2,1)S(1)} %fusion.49, s32[4,2048]{1,0:T(4,128)S(1)} %get-tuple-element.109), kind=kOutput, calls=%fused_computation.18.clone.1 | convolution fusion | flops 542244864 | bytes 1130500 | tf_op jit(solution)/shard_map/while/body/eval_jaxpr/csh,csl->chl/dot_general | solution.py:35
  46.5 3.2 %fusion.48 = f32[4,128,256]{2,1,0:T(8,128)S(1)} fusion(s32[4,2048]{1,0:T(4,128)S(1)} %add_select_fusion.5, bf16[4,2048]{1,0:T(4,128)(2,1)S(1)} %bitcast_convert_fusion.2, s32[4,2048]{1,0:T(4,128)S(1)} %get-tuple-element.109), kind=kOutput, calls=%fused_computation.5.clone.1 | convolution fusion | flops 542113792 | bytes 606208 | tf_op jit(solution)/shard_map/while/body/eval_jaxpr/csh,csl->chl/dot_general | solution.py:32
  49.6 3.8 %fusion.50 = f32[8,4,128,256]{3,2,1,0:T(8,128)} fusion(f32[8,4,128,256]{3,2,1,0:T(8,128)} %get-tuple-element.116, s32[]{:T(128)S(6)} %copy.30, f32[4,128,256]{2,1,0:T(8,128)S(1)} %fusion.48, s32[4,2048]{1,0:T(4,128)S(1)} %add_select_fusion.5, bf16[4,2048]{1,0:T(4,128)(2,1)S(1)} %fusion.49, s32[4,2048]{1,0:T(4,128)S(1)} %get-tuple-element.109), kind=kOutput, calls=%fused_computation.18.clone.1 | convolution fusion | flops 542244864 | bytes 1130500 | tf_op jit(solution)/shard_map/while/body/eval_jaxpr/csh,csl->chl/dot_general | solution.py:35
  53.6 3.2 %fusion.48 = f32[4,128,256]{2,1,0:T(8,128)S(1)} fusion(s32[4,2048]{1,0:T(4,128)S(1)} %add_select_fusion.5, bf16[4,2048]{1,0:T(4,128)(2,1)S(1)} %bitcast_convert_fusion.2, s32[4,2048]{1,0:T(4,128)S(1)} %get-tuple-element.109), kind=kOutput, calls=%fused_computation.5.clone.1 | convolution fusion | flops 542113792 | bytes 606208 | tf_op jit(solution)/shard_map/while/body/eval_jaxpr/csh,csl->chl/dot_general | solution.py:32
  56.7 3.8 %fusion.50 = f32[8,4,128,256]{3,2,1,0:T(8,128)} fusion(f32[8,4,128,256]{3,2,1,0:T(8,128)} %get-tuple-element.116, s32[]{:T(128)S(6)} %copy.30, f32[4,128,256]{2,1,0:T(8,128)S(1)} %fusion.48, s32[4,2048]{1,0:T(4,128)S(1)} %add_select_fusion.5, bf16[4,2048]{1,0:T(4,128)(2,1)S(1)} %fusion.49, s32[4,2048]{1,0:T(4,128)S(1)} %get-tuple-element.109), kind=kOutput, calls=%fused_computation.18.clone.1 | convolution fusion | flops 542244864 | bytes 1130500 | tf_op jit(solution)/shard_map/while/body/eval_jaxpr/csh,csl->chl/dot_general | solution.py:35
  60.7 3.2 %fusion.48 = f32[4,128,256]{2,1,0:T(8,128)S(1)} fusion(s32[4,2048]{1,0:T(4,128)S(1)} %add_select_fusion.5, bf16[4,2048]{1,0:T(4,128)(2,1)S(1)} %bitcast_convert_fusion.2, s32[4,2048]{1,0:T(4,128)S(1)} %get-tuple-element.109), kind=kOutput, calls=%fused_computation.5.clone.1 | convolution fusion | flops 542113792 | bytes 606208 | tf_op jit(solution)/shard_map/while/body/eval_jaxpr/csh,csl->chl/dot_general | solution.py:32
  63.8 3.8 %fusion.50 = f32[8,4,128,256]{3,2,1,0:T(8,128)} fusion(f32[8,4,128,256]{3,2,1,0:T(8,128)} %get-tuple-element.116, s32[]{:T(128)S(6)} %copy.30, f32[4,128,256]{2,1,0:T(8,128)S(1)} %fusion.48, s32[4,2048]{1,0:T(4,128)S(1)} %add_select_fusion.5, bf16[4,2048]{1,0:T(4,128)(2,1)S(1)} %fusion.49, s32[4,2048]{1,0:T(4,128)S(1)} %get-tuple-element.109), kind=kOutput, calls=%fused_computation.18.clone.1 | convolution fusion | flops 542244864 | bytes 1130500 | tf_op jit(solution)/shard_map/while/body/eval_jaxpr/csh,csl->chl/dot_general | solution.py:35
  71.6 4.4 %copy.26 = bf16[4,8,128,256]{3,1,2,0:T(8,128)(2,1)S(1)} copy(f32[4,8,128,256]{3,2,1,0:T(8,128)} %bitcast.62) | data formatting | bytes 6291456
  76.0 6.0 %copy.21 = bf16[32,32768]{0,1:T(8,128)(2,1)} copy(bf16[32,32768]{1,0:T(8,128)(2,1)S(1)} %bitcast.63) | data formatting | bytes 4194304 | tf_op jit(solution)/shard_map/reshape | solution.py:62
  82.0 10.1 %gather_fusion = bf16[2048,32]{1,0:T(8,128)(2,1)S(1)} fusion(bf16[32,32768]{0,1:T(8,128)(2,1)} %copy.21, s32[2048]{0:T(1024)S(1)} %fusion.38), kind=kCustom, calls=%fused_computation | custom fusion | bytes 270336 | tf_op jit(solution)/shard_map/jit(_take)/gather | solution.py:75
  93.0 4.3 %all-to-all-start = ((bf16[32,2,1024]{2,0,1:T(8,128)(2,1)}), bf16[32,2,1024]{2,0,1:T(8,128)(2,1)S(1)}, u32[]{:S(2)}, u32[]{:S(2)}) async-start(bf16[32,2,1024]{2,0,1:T(8,128)(2,1)} %select_convert_fusion), calls=%async_computation | async-start | bytes 262144 | tf_op jit(solution)/shard_map/all_to_all | solution.py:81
  97.3 103.7 %all-reduce.2.cloned.1.call-done = f32[2,32768]{1,0:T(2,128)} async-done(((f32[2,32768]{1,0:T(2,128)}), f32[2,32768]{1,0:T(2,128)}) %all-reduce.2.cloned.1.call-update) | async-done | bytes 262160 | tf_op jit(solution)/shard_map/psum | solution.py:67
  201.0 8.9 %copy.23 = f32[2,32768]{0,1:T(8,128)} copy(f32[2,32768]{1,0:T(2,128)} %all-reduce.2.cloned.1.call-done) | data formatting | bytes 524288 | tf_op jit(solution)/shard_map/psum | solution.py:67
  209.9 11.2 %gather_fusion.1 = f32[2048,2]{1,0:T(8,128)S(1)} fusion(f32[2,32768]{0,1:T(8,128)} %copy.23, s32[2048]{0:T(1024)S(1)} %fusion.38), kind=kCustom, calls=%fused_computation.1 | custom fusion | bytes 40960 | tf_op jit(solution)/shard_map/jit(_take)/gather | solution.py:69
  (61 shorter events, 12.0 us)
Async XLA Ops:
  7.2 193.8 %all-reduce.2.cloned.1.call-start = ((), (), s32[]{:S(2)}) async-start(), calls=%async_computation.1 | async-start | bytes 524288 | tf_op jit(solution)/shard_map/psum | solution.py:67
  67.7 3.9 %copy-start.1 = (s32[2048]{0:T(1024)S(1)}, s32[2048]{0:T(1024)}, u32[]{:S(2)}) copy-start(s32[2048]{0:T(1024)} %param.9) | copy-start | bytes 24580
  93.0 130.2 %all-to-all-start = ((bf16[32,2,1024]{2,0,1:T(8,128)(2,1)}), bf16[32,2,1024]{2,0,1:T(8,128)(2,1)S(1)}, u32[]{:S(2)}, u32[]{:S(2)}) async-start(bf16[32,2,1024]{2,0,1:T(8,128)(2,1)} %select_convert_fusion), calls=%async_computation | async-start | bytes 262144 | tf_op jit(solution)/shard_map/all_to_all | solution.py:81
  201.0 20.5 %copy-start = (f32[2,32768]{1,0:T(2,128)S(1)}, f32[2,32768]{1,0:T(2,128)}, u32[]{:S(2)}) copy-start(f32[2,32768]{1,0:T(2,128)} %all-reduce.2.cloned.1.call-done) | copy-start | bytes 786436
Sparse Core Ops, SparseCore 0:
  71.7 129.2 all-reduce.1
where the time goes:
time: 231 us
  waiting for transfers between devices  104 us (45%)
  matrix products  55.7 us (24%)
  local copies, waits for them, and re-layouts  41.3 us (18%)
  between operations  14.2 us (6%)
  other arithmetic  11.3 us (5%)
  starting transfers between devices  4.31 us (2%)
    psum x1, waiting for transfers between devices, per_device(): sums = lax.psum(terms, ('gx', 'gy', 'gz'))  104 us
    dot_general x8, matrix products, cell_block(): jnp.einsum('csh,csl->chl', high_table, lower_table, preferred_element_typ...  30.5 us
    dot_general x8, matrix products, cell_block(): jnp.einsum('csh,csl->chl', high_table, upper_table, preferred_element_typ...  25.2 us
    gather x1, local copies, waits for them, and re-layouts, per_device(): picked_sums = jnp.take(sums, selected, axis=1)  11.2 us
    gather x2, local copies, waits for them, and re-layouts, per_device(): dense = jnp.take(expanded, selected, axis=1)  10.3 us
    psum x1, local copies, waits for them, and re-layouts, per_device(): sums = lax.psum(terms, ('gx', 'gy', 'gz'))  8.92 us
    reshape x1, local copies, waits for them, and re-layouts, per_device(): expanded = expanded.reshape(local_cells, GENES)  5.99 us
    unnamed x7, local copies, waits for them, and re-layouts  4.7 us
  transfers between devices with their start and end apart: 2, of which 1 were waited for; matrix products, arithmetic and copies ran while one was open for 19% of the time, Pallas kernels for 0%

commit v1 on v0

v1 whole, which is shorter than its diff:
```python
import functools

import jax
import jax.numpy as jnp
from jax import lax
from jax.experimental import pallas as pl
from jax.experimental.pallas import tpu as pltpu
from jax.sharding import PartitionSpec as P

GENES = 32768
BLOCK = 16
LANES = 128

target_sum = 10000.0
var_floor = 0.01
clip_value = 10.0

MESH = pl.DeviceIdType.MESH


def local_kernel(
    owners, columns_ref, counts_ref, nnz_ref, selected_ref, sums_ref, sel_sums_ref, dense_ref,
    value_rows, high_rows, low_rows, offset_rows, block_values, block_offsets, table,
):
    cells, slots = columns_ref.shape
    high_count = GENES // (BLOCK * LANES)
    rows = high_count // owners
    bf16, f32 = jnp.bfloat16, jnp.float32

    sub = lax.broadcasted_iota(jnp.int32, (cells, cells), 0)
    lane = lax.broadcasted_iota(jnp.int32, (cells, cells), 1)
    live_count = jnp.sum(jnp.where(sub == lane, nnz_ref[...], 0), axis=1, keepdims=True)
    slot = lax.broadcasted_iota(jnp.int32, (cells, slots), 1)
    live = slot < live_count
    raw = jnp.where(live, counts_ref[...].astype(f32), 0.0)
    library = jnp.sum(raw, axis=1, keepdims=True)
    value_rows[...] = jnp.log1p(raw * (target_sum / library))
    genes = columns_ref[...]
    high_rows[...] = lax.shift_right_logical(genes, 11).astype(f32)
    low_rows[...] = (lax.shift_right_logical(genes, 4) & (LANES - 1)).astype(f32)
    offset_rows[...] = jnp.where(live, genes & (BLOCK - 1), 0).astype(f32)

    ids = lax.broadcasted_iota(jnp.int32, (16, slots), 0).astype(f32).astype(bf16)

    def spread(ref, c):
        return jnp.broadcast_to(ref[pl.ds(c, 1), :], (16, slots)).astype(bf16)

    def one_cell(c, carry):
        zero, one = bf16(0.0), bf16(1.0)
        hit = spread(high_rows, c) == ids
        left = jnp.concatenate(
            [jnp.where(hit, spread(value_rows, c), zero), jnp.where(hit, spread(offset_rows, c), zero)], axis=0
        )
        low = spread(low_rows, c)
        right = jnp.concatenate(
            [jnp.where(low == ids + bf16(16 * k), one, zero) for k in range(LANES // 16)], axis=0
        )
        placed = lax.dot_general(left, right, (((1,), (1,)), ((), ())), preferred_element_type=f32)
        block_values[c] = placed[:high_count]
        block_offsets[c] = placed[high_count:]
        return carry

    lax.fori_loop(0, cells, one_cell, 0, unroll=2)

    for half in range(high_count // 8):
        span = slice(8 * half, 8 * half + 8)

        def add_cell(c, carry):
            v = block_values[c, span, :]
            o = block_offsets[c, span, :]
            w = v * v
            out = []
            for k in range(BLOCK):
                hit = o == float(k)
                out.append(carry[2 * k] + jnp.where(hit, v, 0.0))
                out.append(carry[2 * k + 1] + jnp.where(hit, w, 0.0))
            return tuple(out)

        parts = lax.fori_loop(0, cells, add_cell, (jnp.zeros((8, LANES), f32),) * (2 * BLOCK))
        for k in range(BLOCK):
            for stat in range(2):
                part = parts[2 * k + stat]
                step = min(rows, 8)
                for first in range(0, 8, step):
                    row = 8 * half + first
                    owner, inner = row // rows, row % rows
                    sums_ref[k * owners + owner, pl.ds(stat * rows + inner, step), :] = part[first:first + step]

    for high in range(high_count):
        cols = slice(high * LANES, (high + 1) * LANES)
        table[0:cells, cols] = block_values[:, high, :].astype(bf16)
        table[cells:, cols] = block_offsets[:, high, :].astype(bf16)

    share = dense_ref.shape[2]
    tiles = share // LANES
    chunk = min(256, share)
    blocks = GENES // BLOCK
    sel_sums_ref[...] = jnp.zeros_like(sel_sums_ref)
    chunk_ids = lax.broadcasted_iota(jnp.int32, (16, chunk), 0).astype(f32).astype(bf16)
    for first in range(0, owners * share, chunk):
        picked = selected_ref[:, first:first + chunk]
        block = lax.shift_right_logical(picked, 4)
        pieces = []
        for group in range(blocks // 256):
            inside = jnp.where(lax.shift_right_logical(block, 8) == group, block & 255, -1).astype(f32)
            inside = jnp.broadcast_to(inside, (16, chunk)).astype(bf16)
            for k in range(16):
                pieces.append(jnp.where(inside == chunk_ids + bf16(16 * k), bf16(1.0), bf16(0.0)))
        found = jnp.dot(table[...], jnp.concatenate(pieces, axis=0), preferred_element_type=f32)
        wanted = (picked & (BLOCK - 1)).astype(f32)
        x = jnp.where(found[cells:] == wanted, found[:cells], 0.0)
        owner, start = first // share, first % share
        dense_ref[owner, :, start:start + chunk] = x.astype(bf16)
        total = jnp.sum(x, axis=0, keepdims=True)
        square = jnp.sum(x * x, axis=0, keepdims=True)
        for stat, line in enumerate((total, square)):
            for tile in range(chunk // LANES):
                r = stat * tiles + start // LANES + tile
                sel_sums_ref[r * owners + owner] = line[:, tile * LANES:(tile + 1) * LANES]


def exchange_kernel(
    sizes, cells, sums_ref, sel_sums_ref, dense_ref, stats_ref, sel_stats_ref, moved_ref,
    got, sel_got, mine, sel_mine, send_sem, recv_sem,
):
    nx, ny, nz = sizes
    teams = nx * ny
    n = teams * nz
    gx, gy, z = lax.axis_index("gx"), lax.axis_index("gy"), lax.axis_index("gz")
    r = gx * ny + gy
    me = r * nz + z

    def place(team, owner):
        return {"gx": lax.div(team, ny), "gy": lax.rem(team, ny), "gz": owner}

    def split(k):
        other = lax.rem(me + k, n)
        return other, place(lax.div(other, nz), lax.rem(other, nz))

    barrier = pltpu.get_barrier_semaphore()

    def greet(k, carry):
        pl.semaphore_signal(barrier, inc=1, device_id=split(k)[1], device_id_type=MESH)
        return carry

    lax.fori_loop(1, n, greet, 0)
    pl.semaphore_wait(barrier, n - 1)

    def send(src, dst, kind, where):
        pltpu.make_async_remote_copy(
            src_ref=src, dst_ref=dst, send_sem=send_sem.at[kind], recv_sem=recv_sem.at[kind],
            device_id=where, device_id_type=MESH,
        ).start()

    def scatter(k, carry):
        other, where = split(k)
        send(sums_ref.at[other], got.at[me], 0, where)
        send(sel_sums_ref.at[other], sel_got.at[me], 1, where)
        return carry

    lax.fori_loop(1, n, scatter, 0)

    def move(k, carry):
        owner = lax.rem(z + k, nz)
        send(dense_ref.at[owner], moved_ref.at[z], 2, place(r, owner))
        return carry

    lax.fori_loop(1, nz, move, 0)

    got[me] = sums_ref[me]
    sel_got[me] = sel_sums_ref[me]
    moved_ref[z] = dense_ref[z]

    def finish(sem, ref, count):
        span = ref.at[pl.ds(0, count)]
        pltpu.make_async_copy(span, span, sem).wait()

    finish(recv_sem.at[0], got, n - 1)
    finish(recv_sem.at[1], sel_got, n - 1)
    rows = mine.shape[0] // 2
    sums = jnp.sum(got[...], axis=0)
    mean = sums[:rows] * (1.0 / cells)
    mine[...] = jnp.concatenate([mean, sums[rows:] * (1.0 / cells) - mean * mean], axis=0)
    sel_mine[...] = jnp.sum(sel_got[...], axis=0)

    def gather(k, carry):
        where = place(lax.rem(r + k, teams), z)
        send(mine, stats_ref.at[r], 3, where)
        send(sel_mine, sel_stats_ref.at[r], 4, where)
        return carry

    lax.fori_loop(1, teams, gather, 0)
    stats_ref[r] = mine[...]
    sel_stats_ref[r] = sel_mine[...]
    finish(recv_sem.at[3], stats_ref, teams - 1)
    finish(recv_sem.at[4], sel_stats_ref, teams - 1)
    finish(recv_sem.at[2], moved_ref, nz - 1)
    finish(send_sem.at[0], got, n - 1)
    finish(send_sem.at[1], sel_got, n - 1)
    finish(send_sem.at[2], moved_ref, nz - 1)
    finish(send_sem.at[3], stats_ref, teams - 1)
    finish(send_sem.at[4], sel_stats_ref, teams - 1)


def final_kernel(cells, stats_ref, sel_stats_ref, moved_ref, gene_ref, pca_ref, turned):
    teams, double, lanes = stats_ref.shape
    rows = double // 2
    for stat in range(2):
        for row in range(rows):
            turned[row * lanes:(row + 1) * lanes, :] = jnp.transpose(stats_ref[:, stat * rows + row, :])
        lines = rows * lanes // 8
        parts = [turned[pl.ds(k, lines, stride=8), :] for k in range(8)]
        gene_ref[:, stat, :] = jnp.concatenate(parts, axis=1)
    owners, local, share = moved_ref.shape
    tiles = share // lanes
    for tile in range(tiles):
        mean = sel_stats_ref[tile] * (1.0 / cells)
        variance = sel_stats_ref[tiles + tile] * (1.0 / cells) - mean * mean
        scale = jnp.sqrt(jnp.maximum(variance, var_floor))
        cols = slice(tile * lanes, (tile + 1) * lanes)
        for owner in range(owners):
            x = moved_ref[owner, :, cols].astype(jnp.float32)
            y = jnp.clip((x - mean) / scale, -clip_value, clip_value)
            pca_ref[owner * local:(owner + 1) * local, cols] = y.astype(jnp.bfloat16)


def per_device(sizes, columns, counts, nnz_count, selected):
    f32, bf16 = jnp.float32, jnp.bfloat16
    nx, ny, owners = sizes
    teams = nx * ny
    n = teams * owners
    local, slots = columns.shape
    cells = local * n
    high_count = GENES // (BLOCK * LANES)
    rows = high_count // owners
    share = selected.shape[0] // owners
    assert teams == BLOCK and rows * owners == high_count and 2 * share // LANES <= teams
    vmem = pl.BlockSpec(memory_space=pltpu.VMEM)
    sums, sel_sums, dense = pl.pallas_call(
        functools.partial(local_kernel, owners),
        name="local_sums",
        out_shape=(
            jax.ShapeDtypeStruct((n, 2 * rows, LANES), f32),
            jax.ShapeDtypeStruct((n, 1, LANES), f32),
            jax.ShapeDtypeStruct((owners, local, share), bf16),
        ),
        in_specs=[vmem] * 4,
        out_specs=(vmem,) * 3,
        scratch_shapes=[pltpu.VMEM((local, slots), f32)] * 4
        + [pltpu.VMEM((local, high_count, LANES), f32)] * 2
        + [pltpu.VMEM((2 * local, GENES // BLOCK), bf16)],
    )(columns, counts, nnz_count.reshape(1, local), selected.reshape(1, -1))
    stats, sel_stats, moved = pl.pallas_call(
        functools.partial(exchange_kernel, sizes, cells),
        name="exchange",
        out_shape=(
            jax.ShapeDtypeStruct((teams, 2 * rows, LANES), f32),
            jax.ShapeDtypeStruct((teams, 1, LANES), f32),
            jax.ShapeDtypeStruct((owners, local, share), bf16),
        ),
        in_specs=[vmem] * 3,
        out_specs=(vmem,) * 3,
        scratch_shapes=[
            pltpu.VMEM((n, 2 * rows, LANES), f32),
            pltpu.VMEM((n, 1, LANES), f32),
            pltpu.VMEM((2 * rows, LANES), f32),
            pltpu.VMEM((1, LANES), f32),
            pltpu.SemaphoreType.DMA((5,)),
            pltpu.SemaphoreType.DMA((5,)),
        ],
        compiler_params=pltpu.CompilerParams(collective_id=0, has_side_effects=True),
    )(sums, sel_sums, dense)
    lines = GENES // owners // LANES
    gene_stats, pca_input = pl.pallas_call(
        functools.partial(final_kernel, cells),
        name="standardize",
        out_shape=(
            jax.ShapeDtypeStruct((lines, 2, LANES), f32),
            jax.ShapeDtypeStruct((owners * local, share), bf16),
        ),
        in_specs=[vmem] * 3,
        out_specs=(vmem,) * 2,
        scratch_shapes=[pltpu.VMEM((rows * LANES, teams), f32)],
    )(stats, sel_stats, moved)
    return (gene_stats.transpose(1, 0, 2).reshape(2, -1), pca_input)


def solution(mesh):
    sizes = tuple(mesh.shape[axis] for axis in ("gx", "gy", "gz"))
    return jax.shard_map(
        functools.partial(per_device, sizes),
        mesh=mesh,
        in_specs=(
            P(("gx", "gy", "gz"), None),
            P(("gx", "gy", "gz"), None),
            P(("gx", "gy", "gz")),
            P(),
        ),
        out_specs=(P(None, "gz"), P(("gx", "gy"), "gz")),
        check_vma=False,
    )
```

time: 231 us -> 37.6 us (0.16)
  waiting for transfers between devices: 104 us -> 0 us
  matrix products: 55.7 us -> 0 us
  local copies, waits for them, and re-layouts: 41.3 us -> 0 us
  Pallas kernels: 0 us -> 36.8 us
  between operations: 14.2 us -> 0.64 us
  other arithmetic: 11.3 us -> 0 us
  starting transfers between devices: 4.31 us -> 0 us
    psum x1 -> x0, waiting for transfers between devices: 104 us -> none  [per_device(): sums = lax.psum(terms, ('gx', 'gy', 'gz'))]
    dot_general x16 -> x0, matrix products: 55.7 us -> none  [the longest x8 30.5 us: cell_block(): jnp.einsum('csh,csl->chl', high_table, lower_table, preferred_element_typ...]
    pallas_call x0 -> x3, Pallas kernels: none -> 36.8 us  [the longest x1 21.6 us: per_device(): pl.pallas_call(functools.partial(exchange_kernel, sizes, cells), name='ex...]
    gather x3 -> x0, local copies, waits for them, and re-layouts: 21.5 us -> none  [the longest x1 11.2 us: per_device(): picked_sums = jnp.take(sums, selected, axis=1)]
    psum x1 -> x0, local copies, waits for them, and re-layouts: 8.92 us -> none  [per_device(): sums = lax.psum(terms, ('gx', 'gy', 'gz'))]
    reshape x3 -> x0, local copies, waits for them, and re-layouts: 6.14 us -> none  [the longest x1 5.99 us: per_device(): expanded = expanded.reshape(local_cells, GENES)]
    unnamed x7 -> x0, local copies, waits for them, and re-layouts: 4.7 us -> none
    all_to_all x1 -> x0, starting transfers between devices: 4.27 us -> none  [per_device(): lax.all_to_all(dense.astype(jnp.bfloat16), 'gz', split_axis=1, concat_axi...]
  transfers between devices with their start and end apart: 2 -> 0, of which waited for: 1 -> 0; matrix products, arithmetic and copies ran while one was open for 19% -> 0% of each run, Pallas kernels for 0% -> 0%
where the time goes in v1:
time: 37.6 us; the launch traced here: 37.4 us
  Pallas kernels  36.8 us (98%)
  between operations  0.64 us (2%)
    pallas_call x1, Pallas kernels, per_device(): pl.pallas_call(functools.partial(exchange_kernel, sizes, cells), name='ex...  21.6 us
    pallas_call x1, Pallas kernels, per_device(): pl.pallas_call(functools.partial(local_kernel, owners), name='local_sums'...  12.8 us
    pallas_call x1, Pallas kernels, per_device(): pl.pallas_call(functools.partial(final_kernel, cells), name='standardize'...  2.33 us

profile of v1, /device:TPU:0, one launch (start us, length us, event | category | flops | bytes accessed | tf_op | source)
XLA Modules:
  0.0 37.4 jit_solution(6131921276529596773)
XLA Ops:
  0.6 12.8 %local_sums.1 = (f32[32,16,128]{2,1,0:T(8,128)}, f32[32,1,128]{2,1,0:T(1,128)}, bf16[2,32,1024]{2,1,0:T(8,128)(2,1)}) custom-call(s32[32,2048]{1,0:T(8,128)} %columns_ref.1, s32[32,2048]{1,0:T(8,128)} %counts_ref.1, s32[1,32]{1,0:T(1,128)} %bitcast.6, s32[1,2048]{1,0:T(1,128)} %bitcast.5), custom_call_target="tpu_custom_call" | custom-call | tf_op jit(solution)/shard_map/local_sums/pallas_call | solution.py:239
  13.4 21.6 %exchange.1 = (f32[16,16,128]{2,1,0:T(8,128)}, f32[16,1,128]{2,1,0:T(1,128)}, bf16[2,32,1024]{2,1,0:T(8,128)(2,1)}) custom-call(f32[32,16,128]{2,1,0:T(8,128)} %get-tuple-element.10.sums_ref, f32[32,1,128]{2,1,0:T(1,128)} %get-tuple-element.11.sel_sums_ref, bf16[2,32,1024]{2,1,0:T(8,128)(2,1)} %get-tuple-element.12.dense_ref), custom_call_target="tpu_custom_call" | custom-call | tf_op jit(solution)/shard_map/exchange/pallas_call | solution.py:253
  35.1 2.3 %standardize.1 = (f32[128,2,128]{2,1,0:T(2,128)}, bf16[64,1024]{1,0:T(8,128)(2,1)}) custom-call(f32[16,16,128]{2,1,0:T(8,128)} %get-tuple-element.13.stats_ref, f32[16,1,128]{2,1,0:T(1,128)} %get-tuple-element.14.sel_stats_ref, bf16[2,32,1024]{2,1,0:T(8,128)(2,1)} %get-tuple-element.15.moved_ref), custom_call_target="tpu_custom_call" | custom-call | tf_op jit(solution)/shard_map/standardize/pallas_call | solution.py:274

commit v2 on v1

--- a/solution.py
+++ b/solution.py
@@ -18,19 +18,52 @@
 MESH = pl.DeviceIdType.MESH
 
 
-def local_kernel(
-    owners, columns_ref, counts_ref, nnz_ref, selected_ref, sums_ref, sel_sums_ref, dense_ref,
+def fused_kernel(
+    sizes, cells, columns_ref, counts_ref, nnz_ref, selected_ref, stats_ref, sel_stats_ref, moved_ref,
     value_rows, high_rows, low_rows, offset_rows, block_values, block_offsets, table,
+    sums_ref, sel_sums_ref, dense_ref, got, sel_got, mine, sel_mine, send_sem, recv_sem,
 ):
-    cells, slots = columns_ref.shape
+    nx, ny, owners = sizes
+    teams = nx * ny
+    n = teams * owners
+    gx, gy, z = lax.axis_index("gx"), lax.axis_index("gy"), lax.axis_index("gz")
+    r = gx * ny + gy
+    me = r * owners + z
+
+    def place(team, owner):
+        return {"gx": lax.div(team, ny), "gy": lax.rem(team, ny), "gz": owner}
+
+    def split(k):
+        other = lax.rem(me + k, n)
+        return other, place(lax.div(other, owners), lax.rem(other, owners))
+
+    barrier = pltpu.get_barrier_semaphore()
+
+    def greet(k, carry):
+        pl.semaphore_signal(barrier, inc=1, device_id=split(k)[1], device_id_type=MESH)
+        return carry
+
+    lax.fori_loop(1, n, greet, 0)
+
+    def send(src, dst, kind, where):
+        pltpu.make_async_remote_copy(
+            src_ref=src, dst_ref=dst, send_sem=send_sem.at[kind], recv_sem=recv_sem.at[kind],
+            device_id=where, device_id_type=MESH,
+        ).start()
+
+    def finish(sem, ref, count):
+        span = ref.at[pl.ds(0, count)]
+        pltpu.make_async_copy(span, span, sem).wait()
+
+    local, slots = columns_ref.shape
     high_count = GENES // (BLOCK * LANES)
     rows = high_count // owners
     bf16, f32 = jnp.bfloat16, jnp.float32
 
-    sub = lax.broadcasted_iota(jnp.int32, (cells, cells), 0)
-    lane = lax.broadcasted_iota(jnp.int32, (cells, cells), 1)
+    sub = lax.broadcasted_iota(jnp.int32, (local, local), 0)
+    lane = lax.broadcasted_iota(jnp.int32, (local, local), 1)
     live_count = jnp.sum(jnp.where(sub == lane, nnz_ref[...], 0), axis=1, keepdims=True)
-    slot = lax.broadcasted_iota(jnp.int32, (cells, slots), 1)
+    slot = lax.broadcasted_iota(jnp.int32, (local, slots), 1)
     live = slot < live_count
     raw = jnp.where(live, counts_ref[...].astype(f32), 0.0)
     library = jnp.sum(raw, axis=1, keepdims=True)
@@ -60,7 +93,7 @@
         block_offsets[c] = placed[high_count:]
         return carry
 
-    lax.fori_loop(0, cells, one_cell, 0, unroll=2)
+    lax.fori_loop(0, local, one_cell, 0, unroll=2)
 
     for half in range(high_count // 8):
         span = slice(8 * half, 8 * half + 8)
@@ -76,7 +109,7 @@
                 out.append(carry[2 * k + 1] + jnp.where(hit, w, 0.0))
             return tuple(out)
 
-        parts = lax.fori_loop(0, cells, add_cell, (jnp.zeros((8, LANES), f32),) * (2 * BLOCK))
+        parts = lax.fori_loop(0, local, add_cell, (jnp.zeros((8, LANES), f32),) * (2 * BLOCK))
         for k in range(BLOCK):
             for stat in range(2):
                 part = parts[2 * k + stat]
@@ -88,8 +121,18 @@
 
     for high in range(high_count):
         cols = slice(high * LANES, (high + 1) * LANES)
-        table[0:cells, cols] = block_values[:, high, :].astype(bf16)
-        table[cells:, cols] = block_offsets[:, high, :].astype(bf16)
+        table[0:local, cols] = block_values[:, high, :].astype(bf16)
+        table[local:, cols] = block_offsets[:, high, :].astype(bf16)
+
+    pl.semaphore_wait(barrier, n - 1)
+
+    def scatter(k, carry):
+        other, where = split(k)
+        send(sums_ref.at[other], got.at[me], 0, where)
+        return carry
+
+    lax.fori_loop(1, n, scatter, 0)
+    got[me] = sums_ref[me]
 
     share = dense_ref.shape[2]
     tiles = share // LANES
@@ -108,96 +151,56 @@
                 pieces.append(jnp.where(inside == chunk_ids + bf16(16 * k), bf16(1.0), bf16(0.0)))
         found = jnp.dot(table[...], jnp.concatenate(pieces, axis=0), preferred_element_type=f32)
         wanted = (picked & (BLOCK - 1)).astype(f32)
-        x = jnp.where(found[cells:] == wanted, found[:cells], 0.0)
+        x = jnp.where(found[local:] == wanted, found[:local], 0.0)
         owner, start = first // share, first % share
         dense_ref[owner, :, start:start + chunk] = x.astype(bf16)
         total = jnp.sum(x, axis=0, keepdims=True)
         square = jnp.sum(x * x, axis=0, keepdims=True)
         for stat, line in enumerate((total, square)):
             for tile in range(chunk // LANES):
-                r = stat * tiles + start // LANES + tile
-                sel_sums_ref[r * owners + owner] = line[:, tile * LANES:(tile + 1) * LANES]
-
-
-def exchange_kernel(
-    sizes, cells, sums_ref, sel_sums_ref, dense_ref, stats_ref, sel_stats_ref, moved_ref,
-    got, sel_got, mine, sel_mine, send_sem, recv_sem,
-):
-    nx, ny, nz = sizes
-    teams = nx * ny
-    n = teams * nz
-    gx, gy, z = lax.axis_index("gx"), lax.axis_index("gy"), lax.axis_index("gz")
-    r = gx * ny + gy
-    me = r * nz + z
-
-    def place(team, owner):
-        return {"gx": lax.div(team, ny), "gy": lax.rem(team, ny), "gz": owner}
-
-    def split(k):
-        other = lax.rem(me + k, n)
-        return other, place(lax.div(other, nz), lax.rem(other, nz))
-
-    barrier = pltpu.get_barrier_semaphore()
-
-    def greet(k, carry):
-        pl.semaphore_signal(barrier, inc=1, device_id=split(k)[1], device_id_type=MESH)
-        return carry
-
-    lax.fori_loop(1, n, greet, 0)
-    pl.semaphore_wait(barrier, n - 1)
-
-    def send(src, dst, kind, where):
-        pltpu.make_async_remote_copy(
-            src_ref=src, dst_ref=dst, send_sem=send_sem.at[kind], recv_sem=recv_sem.at[kind],
-            device_id=where, device_id_type=MESH,
-        ).start()
-
-    def scatter(k, carry):
+                line_row = stat * tiles + start // LANES + tile
+                sel_sums_ref[line_row * owners + owner] = line[:, tile * LANES:(tile + 1) * LANES]
+
+    def move(k, carry):
+        owner = lax.rem(z + k, owners)
+        send(dense_ref.at[owner], moved_ref.at[z], 2, place(r, owner))
+        return carry
+
+    def sel_scatter(k, carry):
         other, where = split(k)
-        send(sums_ref.at[other], got.at[me], 0, where)
         send(sel_sums_ref.at[other], sel_got.at[me], 1, where)
         return carry
 
-    lax.fori_loop(1, n, scatter, 0)
-
-    def move(k, carry):
-        owner = lax.rem(z + k, nz)
-        send(dense_ref.at[owner], moved_ref.at[z], 2, place(r, owner))
-        return carry
-
-    lax.fori_loop(1, nz, move, 0)
-
-    got[me] = sums_ref[me]
+    lax.fori_loop(1, n, sel_scatter, 0)
+    lax.fori_loop(1, owners, move, 0)
     sel_got[me] = sel_sums_ref[me]
     moved_ref[z] = dense_ref[z]
 
-    def finish(sem, ref, count):
-        span = ref.at[pl.ds(0, count)]
-        pltpu.make_async_copy(span, span, sem).wait()
-
     finish(recv_sem.at[0], got, n - 1)
-    finish(recv_sem.at[1], sel_got, n - 1)
-    rows = mine.shape[0] // 2
     sums = jnp.sum(got[...], axis=0)
     mean = sums[:rows] * (1.0 / cells)
     mine[...] = jnp.concatenate([mean, sums[rows:] * (1.0 / cells) - mean * mean], axis=0)
+
+    def gather(k, carry):
+        send(mine, stats_ref.at[r], 3, place(lax.rem(r + k, teams), z))
+        return carry
+
+    def sel_gather(k, carry):
+        send(sel_mine, sel_stats_ref.at[r], 4, place(lax.rem(r + k, teams), z))
+        return carry
+
+    lax.fori_loop(1, teams, gather, 0)
+    finish(recv_sem.at[1], sel_got, n - 1)
     sel_mine[...] = jnp.sum(sel_got[...], axis=0)
-
-    def gather(k, carry):
-        where = place(lax.rem(r + k, teams), z)
-        send(mine, stats_ref.at[r], 3, where)
-        send(sel_mine, sel_stats_ref.at[r], 4, where)
-        return carry
-
-    lax.fori_loop(1, teams, gather, 0)
     stats_ref[r] = mine[...]
+    lax.fori_loop(1, teams, sel_gather, 0)
     sel_stats_ref[r] = sel_mine[...]
+    finish(recv_sem.at[2], moved_ref, owners - 1)
+    finish(send_sem.at[0], got, n - 1)
+    finish(send_sem.at[1], sel_got, n - 1)
+    finish(send_sem.at[2], moved_ref, owners - 1)
     finish(recv_sem.at[3], stats_ref, teams - 1)
     finish(recv_sem.at[4], sel_stats_ref, teams - 1)
-    finish(recv_sem.at[2], moved_ref, nz - 1)
-    finish(send_sem.at[0], got, n - 1)
-    finish(send_sem.at[1], sel_got, n - 1)
-    finish(send_sem.at[2], moved_ref, nz - 1)
     finish(send_sem.at[3], stats_ref, teams - 1)
     finish(send_sem.at[4], sel_stats_ref, teams - 1)
 
@@ -236,31 +239,23 @@
     share = selected.shape[0] // owners
     assert teams == BLOCK and rows * owners == high_count and 2 * share // LANES <= teams
     vmem = pl.BlockSpec(memory_space=pltpu.VMEM)
-    sums, sel_sums, dense = pl.pallas_call(
-        functools.partial(local_kernel, owners),
-        name="local_sums",
+    stats, sel_stats, moved = pl.pallas_call(
+        functools.partial(fused_kernel, sizes, cells),
+        name="sums_and_exchange",
         out_shape=(
-            jax.ShapeDtypeStruct((n, 2 * rows, LANES), f32),
-            jax.ShapeDtypeStruct((n, 1, LANES), f32),
+            jax.ShapeDtypeStruct((teams, 2 * rows, LANES), f32),
+            jax.ShapeDtypeStruct((teams, 1, LANES), f32),
             jax.ShapeDtypeStruct((owners, local, share), bf16),
         ),
         in_specs=[vmem] * 4,
         out_specs=(vmem,) * 3,
         scratch_shapes=[pltpu.VMEM((local, slots), f32)] * 4
         + [pltpu.VMEM((local, high_count, LANES), f32)] * 2
-        + [pltpu.VMEM((2 * local, GENES // BLOCK), bf16)],
-    )(columns, counts, nnz_count.reshape(1, local), selected.reshape(1, -1))
-    stats, sel_stats, moved = pl.pallas_call(
-        functools.partial(exchange_kernel, sizes, cells),
-        name="exchange",
-        out_shape=(
-            jax.ShapeDtypeStruct((teams, 2 * rows, LANES), f32),
-            jax.ShapeDtypeStruct((teams, 1, LANES), f32),
-            jax.ShapeDtypeStruct((owners, local, share), bf16),
-        ),
-        in_specs=[vmem] * 3,
-        out_specs=(vmem,) * 3,
-        scratch_shapes=[
+        + [pltpu.VMEM((2 * local, GENES // BLOCK), bf16)]
+        + [
+            pltpu.VMEM((n, 2 * rows, LANES), f32),
+            pltpu.VMEM((n, 1, LANES), f32),
+            pltpu.VMEM((owners, local, share), bf16),
             pltpu.VMEM((n, 2 * rows, LANES), f32),
             pltpu.VMEM((n, 1, LANES), f32),
             pltpu.VMEM((2 * rows, LANES), f32),
@@ -269,7 +264,7 @@
             pltpu.SemaphoreType.DMA((5,)),
         ],
         compiler_params=pltpu.CompilerParams(collective_id=0, has_side_effects=True),
-    )(sums, sel_sums, dense)
+    )(columns, counts, nnz_count.reshape(1, local), selected.reshape(1, -1))
     lines = GENES // owners // LANES
     gene_stats, pca_input = pl.pallas_call(
         functools.partial(final_kernel, cells),

time: 37.6 us -> 31.8 us (0.85)
  Pallas kernels: 36.8 us -> 31 us
    pallas_call x2 -> x1, Pallas kernels: 34.4 us -> 28.7 us  [per_device(): pl.pallas_call(functools.partial(fused_kernel, sizes, cells), name='sums_...]
where the time goes in v2:
time: 31.8 us; the launch traced here: 31.6 us
  Pallas kernels  31 us (97%)
  between operations  0.64 us (2%)
    pallas_call x1, Pallas kernels, per_device(): pl.pallas_call(functools.partial(fused_kernel, sizes, cells), name='sums_...  28.7 us
    pallas_call x1, Pallas kernels, per_device(): pl.pallas_call(functools.partial(final_kernel, cells), name='standardize'...  2.33 us

profile of v2, /device:TPU:0, one launch (start us, length us, event | category | flops | bytes accessed | tf_op | source)
XLA Modules:
  0.0 31.6 jit_solution(1293651359297783198)
XLA Ops:
  0.6 28.7 %sums_and_exchange.1 = (f32[16,16,128]{2,1,0:T(8,128)}, f32[16,1,128]{2,1,0:T(1,128)}, bf16[2,32,1024]{2,1,0:T(8,128)(2,1)}) custom-call(s32[32,2048]{1,0:T(8,128)} %columns_ref.1, s32[32,2048]{1,0:T(8,128)} %counts_ref.1, s32[1,32]{1,0:T(1,128)} %bitcast.6, s32[1,2048]{1,0:T(1,128)} %bitcast.5), custom_call_target="tpu_custom_call" | custom-call | tf_op jit(solution)/shard_map/sums_and_exchange/pallas_call | solution.py:242
  29.3 2.3 %standardize.1 = (f32[128,2,128]{2,1,0:T(2,128)}, bf16[64,1024]{1,0:T(8,128)(2,1)}) custom-call(f32[16,16,128]{2,1,0:T(8,128)} %get-tuple-element.7.stats_ref, f32[16,1,128]{2,1,0:T(1,128)} %get-tuple-element.8.sel_stats_ref, bf16[2,32,1024]{2,1,0:T(8,128)(2,1)} %get-tuple-element.9.moved_ref), custom_call_target="tpu_custom_call" | custom-call | tf_op jit(solution)/shard_map/standardize/pallas_call | solution.py:269

commit v3 on v2

--- a/solution.py
+++ b/solution.py
@@ -69,8 +69,9 @@
     library = jnp.sum(raw, axis=1, keepdims=True)
     value_rows[...] = jnp.log1p(raw * (target_sum / library))
     genes = columns_ref[...]
-    high_rows[...] = lax.shift_right_logical(genes, 11).astype(f32)
-    low_rows[...] = (lax.shift_right_logical(genes, 4) & (LANES - 1)).astype(f32)
+    upper = (lax.shift_right_logical(genes, 10) & 1) * high_count
+    high_rows[...] = (lax.shift_right_logical(genes, 11) + upper).astype(f32)
+    low_rows[...] = (lax.shift_right_logical(genes, 4) & (LANES // 2 - 1)).astype(f32)
     offset_rows[...] = jnp.where(live, genes & (BLOCK - 1), 0).astype(f32)
 
     ids = lax.broadcasted_iota(jnp.int32, (16, slots), 0).astype(f32).astype(bf16)
@@ -80,20 +81,23 @@
 
     def one_cell(c, carry):
         zero, one = bf16(0.0), bf16(1.0)
-        hit = spread(high_rows, c) == ids
+        high = spread(high_rows, c)
+        hits = [high == ids + bf16(high_count * k) for k in range(2)]
+        value, offset = spread(value_rows, c), spread(offset_rows, c)
         left = jnp.concatenate(
-            [jnp.where(hit, spread(value_rows, c), zero), jnp.where(hit, spread(offset_rows, c), zero)], axis=0
+            [jnp.where(hit, line, zero) for line in (value, offset) for hit in hits], axis=0
         )
         low = spread(low_rows, c)
         right = jnp.concatenate(
-            [jnp.where(low == ids + bf16(16 * k), one, zero) for k in range(LANES // 16)], axis=0
+            [jnp.where(low == ids + bf16(16 * k), one, zero) for k in range(LANES // 32)], axis=0
         )
         placed = lax.dot_general(left, right, (((1,), (1,)), ((), ())), preferred_element_type=f32)
-        block_values[c] = placed[:high_count]
-        block_offsets[c] = placed[high_count:]
-        return carry
-
-    lax.fori_loop(0, local, one_cell, 0, unroll=2)
+        quarters = [placed[high_count * k:high_count * (k + 1)] for k in range(4)]
+        block_values[c] = jnp.concatenate(quarters[:2], axis=1)
+        block_offsets[c] = jnp.concatenate(quarters[2:], axis=1)
+        return carry
+
+    lax.fori_loop(0, local, one_cell, 0, unroll=8)
 
     for half in range(high_count // 8):
         span = slice(8 * half, 8 * half + 8)
@@ -111,13 +115,13 @@
 
         parts = lax.fori_loop(0, local, add_cell, (jnp.zeros((8, LANES), f32),) * (2 * BLOCK))
         for k in range(BLOCK):
-            for stat in range(2):
-                part = parts[2 * k + stat]
-                step = min(rows, 8)
-                for first in range(0, 8, step):
-                    row = 8 * half + first
-                    owner, inner = row // rows, row % rows
-                    sums_ref[k * owners + owner, pl.ds(stat * rows + inner, step), :] = part[first:first + step]
+            near = parts[2 * k] * (1.0 / local)
+            spare = parts[2 * k + 1] - parts[2 * k] * near
+            step = min(rows, 8)
+            for first in range(0, 8, step):
+                owner = (8 * half + first) // rows
+                pair = jnp.concatenate([near[first:first + step], spare[first:first + step]], axis=0)
+                sums_ref[k * owners + owner] = pair.astype(bf16)
 
     for high in range(high_count):
         cols = slice(high * LANES, (high + 1) * LANES)
@@ -177,9 +181,12 @@
     moved_ref[z] = dense_ref[z]
 
     finish(recv_sem.at[0], got, n - 1)
-    sums = jnp.sum(got[...], axis=0)
-    mean = sums[:rows] * (1.0 / cells)
-    mine[...] = jnp.concatenate([mean, sums[rows:] * (1.0 / cells) - mean * mean], axis=0)
+    parts = got[...].astype(f32)
+    means = parts[:, :rows]
+    mean = jnp.sum(means, axis=0) * (1.0 / n)
+    away = means - mean[None]
+    variance = jnp.sum(parts[:, rows:] + (away * away) * float(local), axis=0) * (1.0 / cells)
+    mine[...] = jnp.concatenate([mean, variance], axis=0).astype(bf16)
 
     def gather(k, carry):
         send(mine, stats_ref.at[r], 3, place(lax.rem(r + k, teams), z))
@@ -208,9 +215,10 @@
 def final_kernel(cells, stats_ref, sel_stats_ref, moved_ref, gene_ref, pca_ref, turned):
     teams, double, lanes = stats_ref.shape
     rows = double // 2
+    stats = stats_ref[...].astype(jnp.float32)
     for stat in range(2):
         for row in range(rows):
-            turned[row * lanes:(row + 1) * lanes, :] = jnp.transpose(stats_ref[:, stat * rows + row, :])
+            turned[row * lanes:(row + 1) * lanes, :] = jnp.transpose(stats[:, stat * rows + row, :])
         lines = rows * lanes // 8
         parts = [turned[pl.ds(k, lines, stride=8), :] for k in range(8)]
         gene_ref[:, stat, :] = jnp.concatenate(parts, axis=1)
@@ -237,13 +245,13 @@
     high_count = GENES // (BLOCK * LANES)
     rows = high_count // owners
     share = selected.shape[0] // owners
-    assert teams == BLOCK and rows * owners == high_count and 2 * share // LANES <= teams
+    assert teams == BLOCK and rows * owners == high_count and rows <= 8 and 2 * share // LANES <= teams
     vmem = pl.BlockSpec(memory_space=pltpu.VMEM)
     stats, sel_stats, moved = pl.pallas_call(
         functools.partial(fused_kernel, sizes, cells),
         name="sums_and_exchange",
         out_shape=(
-            jax.ShapeDtypeStruct((teams, 2 * rows, LANES), f32),
+            jax.ShapeDtypeStruct((teams, 2 * rows, LANES), bf16),
             jax.ShapeDtypeStruct((teams, 1, LANES), f32),
             jax.ShapeDtypeStruct((owners, local, share), bf16),
         ),
@@ -253,12 +261,12 @@
         + [pltpu.VMEM((local, high_count, LANES), f32)] * 2
         + [pltpu.VMEM((2 * local, GENES // BLOCK), bf16)]
         + [
-            pltpu.VMEM((n, 2 * rows, LANES), f32),
+            pltpu.VMEM((n, 2 * rows, LANES), bf16),
             pltpu.VMEM((n, 1, LANES), f32),
             pltpu.VMEM((owners, local, share), bf16),
-            pltpu.VMEM((n, 2 * rows, LANES), f32),
+            pltpu.VMEM((n, 2 * rows, LANES), bf16),
             pltpu.VMEM((n, 1, LANES), f32),
-            pltpu.VMEM((2 * rows, LANES), f32),
+            pltpu.VMEM((2 * rows, LANES), bf16),
             pltpu.VMEM((1, LANES), f32),
             pltpu.SemaphoreType.DMA((5,)),
             pltpu.SemaphoreType.DMA((5,)),

time: 31.8 us -> 24.1 us (0.76)
  Pallas kernels: 31 us -> 23.3 us
    pallas_call x1, Pallas kernels: 28.7 us -> 21.1 us  [per_device(): pl.pallas_call(functools.partial(fused_kernel, sizes, cells), name='sums_...]
where the time goes in v3:
time: 24.1 us; the launch traced here: 23.9 us
  Pallas kernels  23.3 us (97%)
  between operations  0.64 us (3%)
    pallas_call x1, Pallas kernels, per_device(): pl.pallas_call(functools.partial(fused_kernel, sizes, cells), name='sums_...  21.1 us
    pallas_call x1, Pallas kernels, per_device(): pl.pallas_call(functools.partial(final_kernel, cells), name='standardize'...  2.2 us

profile of v3, /device:TPU:0, one launch (start us, length us, event | category | flops | bytes accessed | tf_op | source)
XLA Modules:
  0.0 23.9 jit_solution(2846168341804581991)
XLA Ops:
  0.6 21.1 %sums_and_exchange.1 = (bf16[16,16,128]{2,1,0:T(8,128)(2,1)}, f32[16,1,128]{2,1,0:T(1,128)}, bf16[2,32,1024]{2,1,0:T(8,128)(2,1)}) custom-call(s32[32,2048]{1,0:T(8,128)} %columns_ref.1, s32[32,2048]{1,0:T(8,128)} %counts_ref.1, s32[1,32]{1,0:T(1,128)} %bitcast.6, s32[1,2048]{1,0:T(1,128)} %bitcast.5), custom_call_target="tpu_custom_call" | custom-call | tf_op jit(solution)/shard_map/sums_and_exchange/pallas_call | solution.py:250
  21.7 2.2 %standardize.1 = (f32[128,2,128]{2,1,0:T(2,128)}, bf16[64,1024]{1,0:T(8,128)(2,1)}) custom-call(bf16[16,16,128]{2,1,0:T(8,128)(2,1)} %get-tuple-element.7.stats_ref, f32[16,1,128]{2,1,0:T(1,128)} %get-tuple-element.8.sel_stats_ref, bf16[2,32,1024]{2,1,0:T(8,128)(2,1)} %get-tuple-element.9.moved_ref), custom_call_target="tpu_custom_call" | custom-call | tf_op jit(solution)/shard_map/standardize/pallas_call | solution.py:277

commit v4 on v3

--- a/solution.py
+++ b/solution.py
@@ -113,7 +113,7 @@
                 out.append(carry[2 * k + 1] + jnp.where(hit, w, 0.0))
             return tuple(out)
 
-        parts = lax.fori_loop(0, local, add_cell, (jnp.zeros((8, LANES), f32),) * (2 * BLOCK))
+        parts = lax.fori_loop(0, local, add_cell, (jnp.zeros((8, LANES), f32),) * (2 * BLOCK), unroll=4)
         for k in range(BLOCK):
             near = parts[2 * k] * (1.0 / local)
             spare = parts[2 * k + 1] - parts[2 * k] * near

time: 24.1 us -> 23.6 us (0.979)
  Pallas kernels: 23.3 us -> 22.8 us
    pallas_call x1, Pallas kernels: 21.1 us -> 20.6 us  [per_device(): pl.pallas_call(functools.partial(fused_kernel, sizes, cells), name='sums_...]
where the time goes in v4:
time: 23.6 us; the launch traced here: 23.4 us
  Pallas kernels  22.8 us (97%)
  between operations  0.64 us (3%)
    pallas_call x1, Pallas kernels, per_device(): pl.pallas_call(functools.partial(fused_kernel, sizes, cells), name='sums_...  20.6 us
    pallas_call x1, Pallas kernels, per_device(): pl.pallas_call(functools.partial(final_kernel, cells), name='standardize'...  2.2 us

profile of v4, /device:TPU:0, one launch (start us, length us, event | category | flops | bytes accessed | tf_op | source)
XLA Modules:
  0.0 23.4 jit_solution(5211135256692373382)
XLA Ops:
  0.6 20.6 %sums_and_exchange.1 = (bf16[16,16,128]{2,1,0:T(8,128)(2,1)}, f32[16,1,128]{2,1,0:T(1,128)}, bf16[2,32,1024]{2,1,0:T(8,128)(2,1)}) custom-call(s32[32,2048]{1,0:T(8,128)} %columns_ref.1, s32[32,2048]{1,0:T(8,128)} %counts_ref.1, s32[1,32]{1,0:T(1,128)} %bitcast.6, s32[1,2048]{1,0:T(1,128)} %bitcast.5), custom_call_target="tpu_custom_call" | custom-call | tf_op jit(solution)/shard_map/sums_and_exchange/pallas_call | solution.py:250
  21.2 2.2 %standardize.1 = (f32[128,2,128]{2,1,0:T(2,128)}, bf16[64,1024]{1,0:T(8,128)(2,1)}) custom-call(bf16[16,16,128]{2,1,0:T(8,128)(2,1)} %get-tuple-element.7.stats_ref, f32[16,1,128]{2,1,0:T(1,128)} %get-tuple-element.8.sel_stats_ref, bf16[2,32,1024]{2,1,0:T(8,128)(2,1)} %get-tuple-element.9.moved_ref), custom_call_target="tpu_custom_call" | custom-call | tf_op jit(solution)/shard_map/standardize/pallas_call | solution.py:277
